TPU v7x, 32 devices: a whole 2x2x4 slice. The times are simulated.
32 devices in a mesh: data: 4 (over x, y), tp: 8 (over z, core).
Axes of the slice: x: 2, y: 2, z: 4, core: 2. Of those that a mesh axis runs over, the one named last changes fastest.
Arguments:
- x: bfloat16 [16384, 14336], P('data', 'tp'), parts along dimension 0
- w: bfloat16 [14336, 3584], P('tp')
- r: bfloat16 [16384, 3584], P('data'), parts along dimension 0
- g: bfloat16 [3584], replicated
Outputs:
- output: bfloat16 [16384, 3584], P('data'), parts along dimension 0
There are 4 independent parts. A program takes and returns all parts, laid end to end along the dimension named above; an argument that names none is the same for every part.
All inputs are finite; a program needn't handle non-finite values.
Results may differ from a plain program's by a relative error of at most 0.0108131.
Values are sent between devices in bfloat16 or wider.
A program may use at most 1 GiB of HBM per device.

v0:
```python
import jax
import jax.numpy as jnp
from jax import lax
from jax.sharding import PartitionSpec as P

EPS = 1e-6


def solution(mesh):
    tp = mesh.shape["tp"]

    def local(x, w, r, g):
        rows = x.shape[0] // tp
        idx = lax.axis_index("tp")
        p = jnp.dot(x, w, preferred_element_type=jnp.float32).astype(jnp.bfloat16)
        y = lax.psum_scatter(p, "tp", scatter_dimension=0, tiled=True)
        rr = lax.dynamic_slice_in_dim(r, idx * rows, rows, axis=0)
        a = rr.astype(jnp.float32) + y.astype(jnp.float32)
        ms = jnp.mean(a * a, axis=-1, keepdims=True)
        zl = (a * lax.rsqrt(ms + EPS) * g.astype(jnp.float32)).astype(jnp.bfloat16)
        return lax.all_gather(zl, "tp", axis=0, tiled=True)

    return jax.shard_map(
        local,
        mesh=mesh,
        in_specs=(P("data", "tp"), P("tp", None), P("data", None), P(None)),
        out_specs=P("data", None),
        check_vma=False,
    )
```

profile of v0, /device:TPU:0, one launch (start us, length us, event | category | flops | bytes accessed | tf_op | source)
XLA Modules:
  0.0 648.3 jit_solution(14007915542334366001)
XLA Ops:
  6.5 0.0 reduce-scatter.2.cloned.1.call-start
  6.5 61.5 %convolution_convert_fusion = bf16[4096,3584]{1,0:T(8,128)(2,1)} fusion(bf16[4096,1792]{1,0:T(8,128)(2,1)} %param.4, bf16[1792,3584]{1,0:T(8,128)(2,1)} %param.5), kind=kOutput, calls=%fused_computation | convolution fusion | flops 52628029440 | bytes 56885248 | tf_op jit(solution)/shard_map/dot_general | solution.py:15
  68.0 0.0 copy-start.1
  68.0 0.0 reduce-scatter.2.cloned.1.call-update
  68.0 0.0 all-gather.2.cloned.1.call-start
  68.1 0.6 copy-done.1
  68.7 288.6 %reduce-scatter.2.cloned.1.call-done = bf16[512,3584]{1,0:T(8,128)(2,1)} async-done(((bf16[4096,3584]{1,0:T(8,128)(2,1)}), bf16[512,3584]{1,0:T(8,128)(2,1)}) %reduce-scatter.2.cloned.1.call-update) | async-done | bytes 3670032 | tf_op jit(solution)/shard_map/reduce_scatter | solution.py:16
  357.3 0.0 copy-start
  357.3 4.6 multiply_reduce_fusion
  361.9 0.0 copy-done
  361.9 5.6 multiply_convert_fusion
  367.4 0.0 all-gather.2.cloned.1.call-update
  367.5 253.8 %all-gather.2.cloned.1.call-done = bf16[4096,3584]{1,0:T(8,128)(2,1)} async-done(((bf16[512,3584]{1,0:T(8,128)(2,1)}), bf16[4096,3584]{1,0:T(8,128)(2,1)}) %all-gather.2.cloned.1.call-update) | async-done | bytes 29360144 | tf_op jit(solution)/shard_map/all_gather | solution.py:21
  621.3 20.2 %copy.6 = bf16[4096,3584]{1,0:T(8,128)(2,1)} copy(bf16[4096,3584]{1,0:T(8,128)(2,1)} %all-gather.2.cloned.1.call-done) | data formatting | bytes 58720256
  (2 shorter events, 0.0 us)
Async XLA Ops:
  6.5 350.8 %reduce-scatter.2.cloned.1.call-start = ((), (), s32[]{:S(2)}) async-start(), calls=%async_computation.1 | async-start | bytes 33030144 | tf_op jit(solution)/shard_map/reduce_scatter | solution.py:16
  68.0 0.7 copy-start.1
  68.0 553.3 %all-gather.2.cloned.1.call-start = ((), (), s32[]{:S(2)}) async-start(), calls=%async_computation.2 | async-start | bytes 33030144 | tf_op jit(solution)/shard_map/all_gather | solution.py:21
  357.3 4.6 copy-start
Sparse Core Ops, SparseCore 0:
  68.1 289.1 reduce-scatter.1
  367.6 253.6 all-gather.1
where the time goes:
time: 649 us; the launch traced here: 648 us
  waiting for transfers between devices  542 us (84%)
  matrix products  61.5 us (9%)
  local copies, waits for them, and re-layouts  20.8 us (3%)
  between operations  13.4 us (2%)
  other arithmetic  10.1 us (2%)
    reduce_scatter x1, waiting for transfers between devices, local(): y = lax.psum_scatter(p, 'tp', scatter_dimension=0, tiled=True)  289 us
    all_gather x1, waiting for transfers between devices, local(): return lax.all_gather(zl, 'tp', axis=0, tiled=True)  254 us
    dot_general x1, matrix products, local(): p = jnp.dot(x, w, preferred_element_type=jnp.float32).astype(jnp.bfloat16)  61.5 us
    unnamed x5, local copies, waits for them, and re-layouts  20.8 us
  transfers between devices with their start and end apart: 2, of which 2 were waited for; matrix products, arithmetic and copies ran while one was open for 0% of the time, Pallas kernels for 0%

commit v1 on v0

v1 whole, which is shorter than its diff:
```python
import functools

import jax
import jax.numpy as jnp
from jax import lax
from jax.experimental import pallas as pl
from jax.experimental.pallas import tpu as pltpu
from jax.sharding import PartitionSpec as P

EPS = 1e-6
BF = jnp.bfloat16
F32 = jnp.float32

C = 32
Q = 4
NT = 512
PIECE = 512
D = 12
NS = 4
NL = 2
LAGS = (6, 0, 6, 10)


def kernel(
    x_hbm, w_hbm, r_hbm, g_ref, z_ref,
    w_v, x_v, own_v, stage_v, land_v, a_v, b_v, s_v, r_v, f_v,
    w_sem, x_sem, r_sem, dsend, drecv, ssend, arecv, brecv, zrecv, zs_up, zs_dn, zs_d, zdrecv, credit,
):
    rows = z_ref.shape[0]
    half = rows // 2
    hid = z_ref.shape[1]
    mb = C * Q
    nb = half // mb
    nk = half // C
    nt = hid // NT

    me = lax.axis_index("tp")
    core = lax.rem(me, 2)
    zz = lax.div(me, 2)
    p = jnp.where(core == 0, zz, 3 - zz)
    step = 2 - 4 * core
    up, down = me - step, me + step
    partner = me + 1 - 2 * core
    mine = core * half
    other = half - mine
    lag = jnp.where(p == 3, LAGS[3], jnp.where(p == 2, LAGS[2], LAGS[0]))

    def remote(src, dst, send, recv, dev):
        return pltpu.make_async_remote_copy(
            src_ref=src, dst_ref=dst, send_sem=send, recv_sem=recv,
            device_id={"tp": dev}, device_id_type=pl.DeviceIdType.MESH,
        )

    def w_copy(j):
        cols = pl.ds(pl.multiple_of(j * NT, NT), NT)
        return pltpu.make_async_copy(w_hbm.at[:, cols], w_v.at[:, cols], w_sem.at[j])

    def x_copies(b, slot):
        return [
            pltpu.make_async_copy(
                x_hbm.at[pl.ds(pl.multiple_of(base + b * mb, mb), mb)],
                x_v.at[slot, pl.ds(i * mb, mb)],
                x_sem.at[slot, i],
            )
            for i, base in enumerate((mine, other))
        ]

    def r_copy(k):
        return pltpu.make_async_copy(
            r_hbm.at[pl.ds(pl.multiple_of(mine + k * C, C), C)], r_v.at[lax.rem(k, 2)], r_sem.at[lax.rem(k, 2)]
        )

    def stage_copy(b):
        return remote(
            stage_v.at[lax.rem(b, 2)], land_v.at[lax.rem(b, NL)],
            dsend.at[lax.rem(b, 2)], drecv.at[lax.rem(b, NL)], partner,
        )

    def s_copy(k, dst, recv, dev):
        return remote(s_v.at[lax.rem(k, NS)], dst.at[lax.rem(k, D)], ssend.at[lax.rem(k, NS)], recv.at[lax.rem(k, D)], dev)

    def z_rows(k):
        return z_ref.at[pl.ds(pl.multiple_of(mine + k * C, C), C)]

    def z_copy(k, send, recv, dev):
        return remote(z_rows(k), z_rows(k), send, recv, dev)

    def matmul(b):
        slot = lax.rem(b, 2)
        for copy in x_copies(b, slot):
            copy.wait()

        @pl.when(b + 1 < nb)
        def _():
            for copy in x_copies(b + 1, 1 - slot):
                copy.start()

        @pl.when(b >= 2)
        def _():
            stage_copy(b - 2).wait_send()

        def tile(j, carry):
            @pl.when(b == 0)
            def _():
                w_copy(j).wait()

            cols = pl.ds(pl.multiple_of(j * NT, NT), NT)
            acc = jnp.dot(x_v[slot], w_v[:, cols], preferred_element_type=F32)
            own_v[slot, :, cols] = acc[:mb].astype(BF)
            stage_v[slot, :, cols] = acc[mb:].astype(BF)
            return carry

        lax.fori_loop(0, nt, tile, 0)

        @pl.when(b >= NL)
        def _():
            pl.semaphore_wait(credit, 1)

        stage_copy(b).start()

    def send_sum(k, add, dst, recv, dev):
        b, q = lax.div(k, Q), lax.rem(k, Q)
        slot, here, ss = lax.rem(b, 2), pl.ds(pl.multiple_of(q * C, C), C), lax.rem(k, NS)

        @pl.when(k >= NS)
        def _():
            s_copy(k - NS, dst, recv, dev).wait_send()

        for j in range(hid // PIECE):
            cols = pl.ds(j * PIECE, PIECE)
            t = own_v[slot, here, cols].astype(F32) + land_v[lax.rem(b, NL), here, cols].astype(F32)
            if add is not None:
                t += add[lax.rem(k, D), :, cols].astype(F32)
            s_v[ss, :, cols] = t.astype(BF)
        s_copy(k, dst, recv, dev).start()

    def root(k):
        b, q = lax.div(k, Q), lax.rem(k, Q)
        slot, here, ks = lax.rem(b, 2), pl.ds(pl.multiple_of(q * C, C), C), lax.rem(k, D)
        out = pl.ds(pl.multiple_of(mine + k * C, C), C)

        @pl.when(k + 1 < nk)
        def _():
            r_copy(k + 1).start()

        r_copy(k).wait()
        s_copy(k, b_v, brecv, me).wait_recv()
        s_copy(k, a_v, arecv, me).wait_recv()
        ss = jnp.zeros((C, PIECE), F32)
        for j in range(hid // PIECE):
            cols = pl.ds(j * PIECE, PIECE)
            t = own_v[slot, here, cols].astype(F32) + land_v[lax.rem(b, NL), here, cols].astype(F32)
            t += b_v[ks, :, cols].astype(F32)
            t += a_v[ks, :, cols].astype(F32)
            a = r_v[lax.rem(k, 2), :, cols].astype(F32) + t.astype(BF).astype(F32)
            f_v[:, cols] = a
            ss += a * a
        scale = lax.rsqrt(jnp.sum(ss, axis=-1, keepdims=True) * (1.0 / hid) + EPS)
        for j in range(hid // PIECE):
            cols = pl.ds(j * PIECE, PIECE)
            z_ref[out, cols] = (f_v[:, cols] * scale * g_ref[:, cols].astype(F32)).astype(BF)
        z_copy(k, zs_up, zrecv.at[k], up).start()
        z_copy(k, zs_dn, zrecv.at[k], down).start()
        z_copy(k, zs_d, zdrecv, partner).start()

    def pass_on(j):
        @pl.when((p != 1) & (j >= 0))
        def _():
            z_copy(j, zs_d, zrecv.at[j], partner).wait_recv()

            @pl.when(p == 2)
            def _():
                z_copy(j, zs_dn, zrecv.at[j], down).start()

            z_copy(j, zs_d, zdrecv, partner).start()

    def chunk(k, carry):
        b, q = lax.div(k, Q), lax.rem(k, Q)

        @pl.when(q == 0)
        def _():
            stage_copy(b).wait_recv()

        @pl.when(p == 0)
        def _():
            send_sum(k, None, b_v, brecv, down)

        @pl.when(p == 3)
        def _():
            send_sum(k, None, a_v, arecv, up)

        @pl.when(p == 2)
        def _():
            s_copy(k, a_v, arecv, me).wait_recv()
            send_sum(k, a_v, a_v, arecv, up)

        @pl.when(p == 1)
        def _():
            root(k)

        @pl.when((q == Q - 1) & (b < nb - NL))
        def _():
            pl.semaphore_signal(credit, inc=1, device_id={"tp": partner}, device_id_type=pl.DeviceIdType.MESH)

        pass_on(k - lag)

        @pl.when((q == 1) & (b + 1 < nb))
        def _():
            matmul(b + 1)

        return carry

    def drain(k, carry):
        @pl.when(k - lag < nk)
        def _():
            pass_on(k - lag)

        return carry

    for copy in x_copies(0, 0):
        copy.start()

    def w_start(j, carry):
        w_copy(j).start()
        return carry

    lax.fori_loop(0, nt, w_start, 0)

    @pl.when(p == 1)
    def _():
        r_copy(0).start()

    matmul(0)
    lax.fori_loop(0, nk, chunk, 0)
    lax.fori_loop(nk, nk + max(LAGS), drain, 0)

    for b in range(nb - 2, nb):
        stage_copy(b).wait_send()

    @pl.when(p != 1)
    def _():
        for k in range(nk - NS, nk):
            s_copy(k, a_v, arecv, me).wait_send()

    def whole(base, send, recv):
        ref = z_ref.at[pl.ds(pl.multiple_of(base, half), half)]
        return remote(ref, ref, send, recv, partner)

    @pl.when(p == 1)
    def _():
        whole(mine, zs_up, zdrecv).wait_send()

    @pl.when((p == 1) | (p == 2))
    def _():
        whole(mine, zs_dn, zdrecv).wait_send()

    whole(mine, zs_d, zdrecv).wait_send()
    whole(other, zs_d, zdrecv).wait_recv()


def solution(mesh):
    assert mesh.shape["tp"] == 8

    def local(x, w, r, g):
        rows, depth = x.shape
        hid = w.shape[1]
        half = rows // 2
        mb = C * Q
        nk = half // C
        anyspace = pl.BlockSpec(memory_space=pl.ANY)
        vmem = pl.BlockSpec(memory_space=pltpu.VMEM)
        dma = pltpu.SemaphoreType.DMA
        return pl.pallas_call(
            kernel,
            out_shape=jax.ShapeDtypeStruct((rows, hid), BF),
            in_specs=[anyspace, anyspace, anyspace, vmem],
            out_specs=vmem,
            scratch_shapes=[
                pltpu.VMEM((depth, hid), BF),
                pltpu.VMEM((2, 2 * mb, depth), BF),
                pltpu.VMEM((2, mb, hid), BF),
                pltpu.VMEM((2, mb, hid), BF),
                pltpu.VMEM((NL, mb, hid), BF),
                pltpu.VMEM((D, C, hid), BF),
                pltpu.VMEM((D, C, hid), BF),
                pltpu.VMEM((NS, C, hid), BF),
                pltpu.VMEM((2, C, hid), BF),
                pltpu.VMEM((C, hid), F32),
                dma((hid // NT,)),
                dma((2, 2)),
                dma((2,)),
                dma((2,)),
                dma((NL,)),
                dma((NS,)),
                dma((D,)),
                dma((D,)),
                dma((nk,)),
                dma,
                dma,
                dma,
                dma,
                pltpu.SemaphoreType.REGULAR,
            ],
            compiler_params=pltpu.CompilerParams(has_side_effects=True, vmem_limit_bytes=67043328),
            cost_estimate=pl.CostEstimate(
                flops=2 * rows * depth * hid,
                bytes_accessed=2 * (rows * depth + depth * hid + 2 * rows * hid),
                transcendentals=rows,
            ),
        )(x, w, r, g.reshape(1, hid))

    return jax.shard_map(
        local,
        mesh=mesh,
        in_specs=(P("data", "tp"), P("tp", None), P("data", None), P(None)),
        out_specs=P("data", None),
        check_vma=False,
    )
```

time: 649 us -> 394 us (0.61)
  waiting for transfers between devices: 542 us -> 0 us
  Pallas kernels: 0 us -> 372 us
  matrix products: 61.5 us -> 0 us
  between operations: 13.4 us -> 0.01 us
  other arithmetic: 10.1 us -> 0 us
    pallas_call x0 -> x1, Pallas kernels: none -> 372 us  [local(): pl.pallas_call(kernel, out_shape=jax.ShapeDtypeStruct((rows, hid), BF), i...]
    reduce_scatter x1 -> x0, waiting for transfers between devices: 289 us -> none  [local(): y = lax.psum_scatter(p, 'tp', scatter_dimension=0, tiled=True)]
    all_gather x1 -> x0, waiting for transfers between devices: 254 us -> none  [local(): return lax.all_gather(zl, 'tp', axis=0, tiled=True)]
    dot_general x1 -> x0, matrix products: 61.5 us -> none  [local(): p = jnp.dot(x, w, preferred_element_type=jnp.float32).astype(jnp.bfloat16)]
    unnamed x5 -> x1, local copies, waits for them, and re-layouts: 20.8 us -> 20.4 us
  transfers between devices with their start and end apart: 2 -> 0, of which waited for: 2 -> 0; matrix products, arithmetic and copies ran while one was open for 0% -> 0% of each run, Pallas kernels for 0% -> 0%
where the time goes in v1:
time: 394 us
  Pallas kernels  372 us (94%)
  local copies, waits for them, and re-layouts  21.8 us (6%)
    pallas_call x1, Pallas kernels, local(): pl.pallas_call(kernel, out_shape=jax.ShapeDtypeStruct((rows, hid), BF), i...  372 us
    unnamed x1, local copies, waits for them, and re-layouts  20.4 us

profile of v1, /device:TPU:0, one launch (start us, length us, event | category | flops | bytes accessed | tf_op | source)
XLA Modules:
  0.0 393.6 jit_solution(17335770130512388354)
XLA Ops:
  0.0 1.3 reshape.3.g_ref
  1.3 371.9 %shard_map.46 = bf16[4096,3584]{1,0:T(8,128)(2,1)} custom-call(bf16[4096,1792]{1,0:T(8,128)(2,1)} %x_hbm.1, bf16[1792,3584]{1,0:T(8,128)(2,1)} %w_hbm.1, bf16[4096,3584]{1,0:T(8,128)(2,1)} %r_hbm.1, bf16[1,3584]{1,0:T(2,128)(2,1)} %reshape.3.g_ref), custom_call_target="tpu_custom_call" | custom-call | flops 52613349376 | bytes 86245376 | tf_op jit(solution)/shard_map/pallas_call | solution.py:273
  373.2 20.4 %copy.6 = bf16[4096,3584]{1,0:T(8,128)(2,1)} copy(bf16[4096,3584]{1,0:T(8,128)(2,1)} %shard_map.46) | data formatting | bytes 58720256

commit v2 on v1

--- a/solution.py
+++ b/solution.py
@@ -11,20 +11,22 @@
 BF = jnp.bfloat16
 F32 = jnp.float32
 
-C = 32
-Q = 4
+C = 16
+Q = 8
 NT = 512
 PIECE = 512
-D = 12
-NS = 4
-NL = 2
-LAGS = (6, 0, 6, 10)
+D = 20
+NS = 8
+NL = 3
+LAGS = (12, 0, 4, 14)
+TQ = 2
+OUT = 8
 
 
 def kernel(
-    x_hbm, w_hbm, r_hbm, g_ref, z_ref,
-    w_v, x_v, own_v, stage_v, land_v, a_v, b_v, s_v, r_v, f_v,
-    w_sem, x_sem, r_sem, dsend, drecv, ssend, arecv, brecv, zrecv, zs_up, zs_dn, zs_d, zdrecv, credit,
+    x_hbm, w_hbm, r_hbm, g_hbm, z_ref,
+    w_v, x_v, own_v, stage_v, land_v, a_v, b_v, s_v, r_v, f_v, g_v, g_raw,
+    w_sem, x_sem, r_sem, dsend, drecv, ssend, arecv, brecv, zrecv, zs_up, zs_dn, zs_d, zdrecv, g_sem, credit,
 ):
     rows = z_ref.shape[0]
     half = rows // 2
@@ -43,6 +45,7 @@
     partner = me + 1 - 2 * core
     mine = core * half
     other = half - mine
+    leaf = (p == 0) | (p == 3)
     lag = jnp.where(p == 3, LAGS[3], jnp.where(p == 2, LAGS[2], LAGS[0]))
 
     def remote(src, dst, send, recv, dev):
@@ -70,11 +73,9 @@
             r_hbm.at[pl.ds(pl.multiple_of(mine + k * C, C), C)], r_v.at[lax.rem(k, 2)], r_sem.at[lax.rem(k, 2)]
         )
 
-    def stage_copy(b):
-        return remote(
-            stage_v.at[lax.rem(b, 2)], land_v.at[lax.rem(b, NL)],
-            dsend.at[lax.rem(b, 2)], drecv.at[lax.rem(b, NL)], partner,
-        )
+    def stage_copy(b, cols=slice(None)):
+        slot, there = lax.rem(b, 2), lax.rem(b, NL)
+        return remote(stage_v.at[slot, :, cols], land_v.at[there, :, cols], dsend.at[slot], drecv.at[there], partner)
 
     def s_copy(k, dst, recv, dev):
         return remote(s_v.at[lax.rem(k, NS)], dst.at[lax.rem(k, D)], ssend.at[lax.rem(k, NS)], recv.at[lax.rem(k, D)], dev)
@@ -85,7 +86,7 @@
     def z_copy(k, send, recv, dev):
         return remote(z_rows(k), z_rows(k), send, recv, dev)
 
-    def matmul(b):
+    def open_block(b):
         slot = lax.rem(b, 2)
         for copy in x_copies(b, slot):
             copy.wait()
@@ -99,24 +100,30 @@
         def _():
             stage_copy(b - 2).wait_send()
 
-        def tile(j, carry):
-            @pl.when(b == 0)
+        @pl.when(b >= NL)
+        def _():
+            pl.semaphore_wait(credit, 1)
+
+    def tile(b, j, ready=None):
+        slot = lax.rem(b, 2)
+        cols = pl.ds(pl.multiple_of(j * NT, NT), NT)
+        acc = jnp.dot(x_v[slot], w_v[:, cols], preferred_element_type=F32)
+        stage_v[slot, :, cols] = acc[mb:].astype(BF)
+        own_v[slot, :, cols] = acc[:mb].astype(BF)
+        if ready is not None:
+            ready()
+        stage_copy(b, cols).start()
+
+    def tiles(b, q):
+        @pl.when((b < nb) & (q == 0))
+        def _():
+            open_block(b)
+
+        for i in range(TQ):
+
+            @pl.when((b < nb) & (q * TQ + i < nt))
             def _():
-                w_copy(j).wait()
-
-            cols = pl.ds(pl.multiple_of(j * NT, NT), NT)
-            acc = jnp.dot(x_v[slot], w_v[:, cols], preferred_element_type=F32)
-            own_v[slot, :, cols] = acc[:mb].astype(BF)
-            stage_v[slot, :, cols] = acc[mb:].astype(BF)
-            return carry
-
-        lax.fori_loop(0, nt, tile, 0)
-
-        @pl.when(b >= NL)
-        def _():
-            pl.semaphore_wait(credit, 1)
-
-        stage_copy(b).start()
+                tile(b, q * TQ + i)
 
     def send_sum(k, add, dst, recv, dev):
         b, q = lax.div(k, Q), lax.rem(k, Q)
@@ -158,7 +165,7 @@
         scale = lax.rsqrt(jnp.sum(ss, axis=-1, keepdims=True) * (1.0 / hid) + EPS)
         for j in range(hid // PIECE):
             cols = pl.ds(j * PIECE, PIECE)
-            z_ref[out, cols] = (f_v[:, cols] * scale * g_ref[:, cols].astype(F32)).astype(BF)
+            z_ref[out, cols] = (f_v[:, cols] * scale * g_v[:, cols]).astype(BF)
         z_copy(k, zs_up, zrecv.at[k], up).start()
         z_copy(k, zs_dn, zrecv.at[k], down).start()
         z_copy(k, zs_d, zdrecv, partner).start()
@@ -177,6 +184,10 @@
     def chunk(k, carry):
         b, q = lax.div(k, Q), lax.rem(k, Q)
 
+        @pl.when(jnp.logical_not(leaf))
+        def _():
+            tiles(b + 1, q)
+
         @pl.when(q == 0)
         def _():
             stage_copy(b).wait_recv()
@@ -204,9 +215,9 @@
 
         pass_on(k - lag)
 
-        @pl.when((q == 1) & (b + 1 < nb))
-        def _():
-            matmul(b + 1)
+        @pl.when(leaf)
+        def _():
+            tiles(b + 1, q)
 
         return carry
 
@@ -225,12 +236,46 @@
         return carry
 
     lax.fori_loop(0, nt, w_start, 0)
+    g_copy = pltpu.make_async_copy(g_hbm, g_raw, g_sem)
+    g_copy.start()
 
     @pl.when(p == 1)
     def _():
         r_copy(0).start()
 
-    matmul(0)
+    barrier = pltpu.get_barrier_semaphore()
+
+    def greet(dev):
+        pl.semaphore_signal(barrier, inc=1, device_id={"tp": dev}, device_id_type=pl.DeviceIdType.MESH)
+
+    greet(partner)
+
+    @pl.when(p != 0)
+    def _():
+        greet(up)
+
+    @pl.when(p != 3)
+    def _():
+        greet(down)
+
+    open_block(0)
+
+    def met():
+        pl.semaphore_wait(barrier, jnp.where(leaf, 2, 3))
+
+    w_copy(0).wait()
+    tile(0, 0, met)
+
+    def first(j, carry):
+        w_copy(j).wait()
+        tile(0, j)
+        return carry
+
+    lax.fori_loop(1, nt, first, 0)
+    g_copy.wait()
+    for j in range(hid // PIECE):
+        cols = pl.ds(j * PIECE, PIECE)
+        g_v[:, cols] = g_raw[cols].astype(F32).reshape(1, PIECE)
     lax.fori_loop(0, nk, chunk, 0)
     lax.fori_loop(nk, nk + max(LAGS), drain, 0)
 
@@ -256,6 +301,18 @@
 
     whole(mine, zs_d, zdrecv).wait_send()
     whole(other, zs_d, zdrecv).wait_recv()
+
+
+def put(n, z_ref, out_ref, sem):
+    rows = z_ref.shape[0] // n
+    copies = [
+        pltpu.make_async_copy(z_ref.at[pl.ds(i * rows, rows)], out_ref.at[pl.ds(i * rows, rows)], sem.at[i])
+        for i in range(n)
+    ]
+    for copy in copies:
+        copy.start()
+    for copy in copies:
+        copy.wait()
 
 
 def solution(mesh):
@@ -270,10 +327,10 @@
         anyspace = pl.BlockSpec(memory_space=pl.ANY)
         vmem = pl.BlockSpec(memory_space=pltpu.VMEM)
         dma = pltpu.SemaphoreType.DMA
-        return pl.pallas_call(
+        z = pl.pallas_call(
             kernel,
-            out_shape=jax.ShapeDtypeStruct((rows, hid), BF),
-            in_specs=[anyspace, anyspace, anyspace, vmem],
+            out_shape=pltpu.VMEM((rows, hid), BF),
+            in_specs=[anyspace, anyspace, anyspace, anyspace],
             out_specs=vmem,
             scratch_shapes=[
                 pltpu.VMEM((depth, hid), BF),
@@ -286,6 +343,8 @@
                 pltpu.VMEM((NS, C, hid), BF),
                 pltpu.VMEM((2, C, hid), BF),
                 pltpu.VMEM((C, hid), F32),
+                pltpu.VMEM((1, hid), F32),
+                pltpu.VMEM((hid,), BF),
                 dma((hid // NT,)),
                 dma((2, 2)),
                 dma((2,)),
@@ -299,15 +358,24 @@
                 dma,
                 dma,
                 dma,
+                dma,
                 pltpu.SemaphoreType.REGULAR,
             ],
-            compiler_params=pltpu.CompilerParams(has_side_effects=True, vmem_limit_bytes=67043328),
+            compiler_params=pltpu.CompilerParams(has_side_effects=True, collective_id=0, vmem_limit_bytes=34 * 2**20),
             cost_estimate=pl.CostEstimate(
                 flops=2 * rows * depth * hid,
                 bytes_accessed=2 * (rows * depth + depth * hid + 2 * rows * hid),
                 transcendentals=rows,
             ),
-        )(x, w, r, g.reshape(1, hid))
+        )(x, w, r, g)
+        return pl.pallas_call(
+            functools.partial(put, OUT),
+            out_shape=jax.ShapeDtypeStruct((rows, hid), BF),
+            in_specs=[vmem],
+            out_specs=anyspace,
+            scratch_shapes=[dma((OUT,))],
+            compiler_params=pltpu.CompilerParams(vmem_limit_bytes=2**20),
+        )(z)
 
     return jax.shard_map(
         local,

time: 394 us -> 350 us (0.89)
  Pallas kernels: 372 us -> 350 us
  local copies, waits for them, and re-layouts: 21.8 us -> 0 us
    pallas_call x1 -> x2, Pallas kernels: 372 us -> 350 us  [the longest x1 340 us: local(): pl.pallas_call(kernel, out_shape=pltpu.VMEM((rows, hid), BF), in_specs=[a...]
    unnamed x1 -> x0, local copies, waits for them, and re-layouts: 20.4 us -> none
where the time goes in v2:
time: 350 us
  Pallas kernels  350 us (100%)
    pallas_call x1, Pallas kernels, local(): pl.pallas_call(kernel, out_shape=pltpu.VMEM((rows, hid), BF), in_specs=[a...  340 us
    pallas_call x1, Pallas kernels, local(): pl.pallas_call(functools.partial(put, OUT), out_shape=jax.ShapeDtypeStruc...  9.84 us

profile of v2, /device:TPU:0, one launch (start us, length us, event | category | flops | bytes accessed | tf_op | source)
XLA Modules:
  0.0 350.1 jit_solution(7244815245503046200)
XLA Ops:
  0.0 340.3 %shard_map.46.z_ref = bf16[4096,3584]{1,0:T(8,128)(2,1)S(1)} custom-call(bf16[4096,1792]{1,0:T(8,128)(2,1)} %x_hbm.1, bf16[1792,3584]{1,0:T(8,128)(2,1)} %w_hbm.1, bf16[4096,3584]{1,0:T(8,128)(2,1)} %r_hbm.1, bf16[3584]{0:T(1024)(128)(2,1)} %g_hbm.1), custom_call_target="tpu_custom_call" | custom-call | flops 52613349376 | bytes 86245376 | tf_op jit(solution)/shard_map/pallas_call | solution.py:330
  340.3 9.8 %shard_map.47 = bf16[4096,3584]{1,0:T(8,128)(2,1)} custom-call(bf16[4096,3584]{1,0:T(8,128)(2,1)S(1)} %shard_map.46.z_ref), custom_call_target="tpu_custom_call" | custom-call | tf_op jit(solution)/shard_map/pallas_call | solution.py:371
